TPU v7x, 128 devices: a whole 4x4x4 slice. The times are simulated.
128 devices in a mesh: ctx: 16 (over z_hi, y, core), tp: 8 (over x, z_lo).
Axes of the slice: x: 4, y: 4, z: 4 (z_hi: 2, z_lo: 2; z = z_hi * 2 + z_lo), core: 2. Of those that a mesh axis runs over, the one named last changes fastest.
Arguments:
- hidden: bfloat16 [16384, 4096], P('ctx'), may hold values from -6 to 6
- norm_gain: float32 [4096], replicated, may hold values from 0.25 to 1.75
- w_query: bfloat16 [4096, 4096], P(None, 'tp')
- w_key: bfloat16 [4096, 1024], P(None, 'tp')
- w_value: bfloat16 [4096, 1024], P(None, 'tp'), may hold values from -0.09375 to 0.09375
- w_output: bfloat16 [4096, 4096], P('tp'), may hold values from -0.09375 to 0.09375
- positions: int32 [8192], P('ctx'), may hold values from -1 to 16383, as said below
- counts: int32 [64], P('ctx'), may hold values from 1 to 128, as said below
- router_weight: float32 [16384], P('ctx'), may hold values from 0.25 to 2
Outputs:
- mixed: bfloat16 [16384, 4096], P('ctx', 'tp')
Inputs may be any that keep to these rules, and one draw needn't show every extreme that they name: Slots of ctx index s are those from s * 512 to (s + 1) * 512 - 1; their live slots hold distinct positions from s * 1024 to (s + 1) * 1024 - 1, increasing in slot order; other slots hold -1. `counts`: blocks of ctx index s are those from s * 4 to (s + 1) * 4 - 1; one block among all 64 is full.
All inputs are finite; a program needn't handle non-finite values.
Results may differ from a plain program's by a relative error of at most 0.0089.
Values may be sent and summed in bfloat16 or wider, within the bound.
A program may use at most 128 MiB of HBM per device.

v0:
```python
import jax
import jax.numpy as jnp
from jax import lax
from jax.sharding import Mesh
from jax.sharding import PartitionSpec as P

HEAD_DIM = 128
BLOCK = 128
CTX = ("ctx_0", "ctx_1", "ctx_2")


def gathered_by_axis(value, axes, dim):
    if not axes:
        return value
    nearer = lax.all_gather(value, axes[-1], axis=dim, tiled=True)
    return gathered_by_axis(nearer, axes[:-1], dim)


def cut_along(value, dim, devices):
    shape = value.shape
    parts = value.reshape(*shape[:dim], devices, shape[dim] // devices, *shape[dim + 1 :])
    return jnp.moveaxis(parts, dim, 0)


def sent_and_summed(value, axis, dim):
    parts = cut_along(value, dim, lax.axis_size(axis))
    arrived = lax.all_to_all(parts, axis, split_axis=0, concat_axis=0, tiled=True)
    return arrived.astype(jnp.float32).sum(axis=0)


def rotate(field, angle_pos):
    half = field.shape[-1] // 2
    freq = 500000.0 ** (-2.0 * jnp.arange(half, dtype=jnp.float32) / field.shape[-1])
    angle = angle_pos[:, None] * freq[None, :]
    cosine = jnp.cos(angle)[:, None, :]
    sine = jnp.sin(angle)[:, None, :]
    first = field[..., :half]
    second = field[..., half:]
    return jnp.concatenate(
        [first * cosine - second * sine, second * cosine + first * sine], axis=-1
    )


def attend(queries, query_pos, key_rows, value_rows, key_pos):
    slot_count, kv_here, group, head_dim = queries.shape
    start_best = jnp.full((kv_here, group, slot_count), -1e30, jnp.float32)
    start_total = jnp.zeros((kv_here, group, slot_count), jnp.float32)
    start_acc = jnp.zeros((kv_here, group, slot_count, head_dim), jnp.float32)
    latest = jnp.max(query_pos)

    def block_step(carry, block):
        best, total, accum = carry
        block_keys, block_values, block_pos = block
        score = jnp.einsum(
            "qkgd,nkd->kgqn", queries, block_keys, preferred_element_type=jnp.float32
        ) * head_dim ** (-0.5)
        allowed = (block_pos[None, :] <= query_pos[:, None])[None, None, :, :]
        masked = jnp.where(allowed, score, -1e30)
        new_best = jnp.maximum(best, jnp.max(masked, axis=-1))
        factor = jnp.exp(best - new_best)
        weight = jnp.where(allowed, jnp.exp(masked - new_best[..., None]), 0.0)
        total = total * factor + jnp.sum(weight, axis=-1)
        product = jnp.einsum(
            "kgqn,nkd->kgqd",
            weight.astype(jnp.bfloat16),
            block_values,
            preferred_element_type=jnp.float32,
        )
        accum = accum * factor[..., None] + product
        return (new_best, total, accum)

    piece_keys = gathered_by_axis(key_rows, ("ctx_2", "ctx_1", "ctx_0"), 0)
    piece_values = gathered_by_axis(value_rows, ("ctx_2", "ctx_1", "ctx_0"), 0)
    piece_pos = gathered_by_axis(key_pos, ("ctx_2", "ctx_1", "ctx_0"), 0)
    length = piece_keys.shape[0]

    def compute(state):
        if length > 512 and length % 512 == 0:
            steps_count = length // 512
            blocks = (
                piece_keys.reshape(steps_count, 512, kv_here, head_dim),
                piece_values.reshape(steps_count, 512, kv_here, head_dim),
                piece_pos.reshape(steps_count, 512),
            )
            result, unused = lax.scan(
                lambda inner, block: (block_step(inner, block), None), state, blocks
            )
            return result
        return block_step(state, (piece_keys, piece_values, piece_pos))

    best, total, accum = lax.cond(
        jnp.min(piece_pos) <= latest,
        compute,
        lambda state: state,
        (start_best, start_total, start_acc),
    )
    total = jnp.where(total > 0, total, 1.0)
    result = (accum / total[..., None]).astype(jnp.bfloat16)
    return jnp.transpose(result, (2, 0, 1, 3)).reshape(slot_count, kv_here * group * head_dim)


def per_device(
    hidden, norm_gain, w_query, w_key, w_value, w_output, positions, counts, router_weight
):
    seq_here = hidden.shape[0]
    slot_count = positions.shape[0]
    shard = lax.axis_index(CTX)
    within = jnp.arange(slot_count, dtype=jnp.int32)
    live = within % BLOCK < jnp.repeat(counts, BLOCK, total_repeat_length=slot_count)
    local_pos = positions - shard * seq_here
    index = jnp.where(live, local_pos, 0)
    rows = hidden[index].astype(jnp.float32) * live[:, None].astype(jnp.float32)
    scale_rows = lax.rsqrt(jnp.mean(rows * rows, axis=-1, keepdims=True) + 1e-05)
    normed = (rows * scale_rows * norm_gain[None, :]).astype(jnp.bfloat16)
    heads_here = w_query.shape[1] // HEAD_DIM
    kv_here = w_key.shape[1] // HEAD_DIM
    group = heads_here // kv_here
    queries = jnp.dot(normed, w_query, preferred_element_type=jnp.float32)
    key_rows = jnp.dot(normed, w_key, preferred_element_type=jnp.float32)
    value_rows = jnp.dot(normed, w_value, preferred_element_type=jnp.float32).astype(jnp.bfloat16)
    angle_pos = jnp.where(live, positions, 0).astype(jnp.float32)
    queries = rotate(queries.reshape(slot_count, heads_here, HEAD_DIM), angle_pos).astype(
        jnp.bfloat16
    )
    queries = queries.reshape(slot_count, kv_here, group, HEAD_DIM)
    key_rows = rotate(key_rows.reshape(slot_count, kv_here, HEAD_DIM), angle_pos).astype(
        jnp.bfloat16
    )
    value_rows = value_rows.reshape(slot_count, kv_here, HEAD_DIM)
    query_pos = jnp.where(live, positions, -1)
    key_pos = jnp.where(live, positions, 2**30)
    attn = attend(queries, query_pos, key_rows, value_rows, key_pos)
    partial_proj = jnp.dot(attn, w_output, preferred_element_type=jnp.float32)
    summed = sent_and_summed(partial_proj.astype(jnp.bfloat16), "tp", 1)
    width = summed.shape[1]
    own_cols = lax.dynamic_slice_in_dim(hidden, lax.axis_index("tp") * width, width, 1).astype(
        jnp.float32
    )
    target = jnp.where(live, local_pos, seq_here)
    update = router_weight[index][:, None] * summed
    mixed = own_cols.at[target].add(update, mode="drop")
    return mixed.astype(jnp.bfloat16)


def solution(mesh):
    finer = Mesh(mesh.devices.reshape(2, 4, 2, mesh.shape["tp"]), ("ctx_0", "ctx_1", "ctx_2", "tp"))
    return jax.shard_map(
        per_device,
        mesh=finer,
        in_specs=(
            P(CTX, None),
            P(),
            P(None, "tp"),
            P(None, "tp"),
            P(None, "tp"),
            P("tp", None),
            P(CTX),
            P(CTX),
            P(CTX),
        ),
        out_specs=P(CTX, "tp"),
        check_vma=False,
    )
```

profile of v0, /device:TPU:88, one launch (start us, length us, event | category | flops | bytes accessed | tf_op | source)
XLA Modules:
  0.0 388.5 jit_solution(13800304367469875257)
XLA Ops:
  6.6 1.5 fusion.48
  8.0 2.5 compare_select_fusion.2
  11.2 1.3 fusion.46
  12.5 13.0 %gather_fusion.1 = bf16[512,4096]{1,0:T(8,128)(2,1)} fusion(bf16[1024,4096]{1,0:T(8,128)(2,1)} %param.15, s32[1024]{0:T(1024)S(1)} %pad_clamp_fusion), kind=kCustom, calls=%fused_computation.1 | custom fusion | bytes 8390656 | tf_op jit(solution)/shard_map/gather | solution.py:112
  25.6 3.6 multiply_reduce_fusion
  29.2 2.3 multiply_convert_fusion
  31.5 1.9 copy-done.5
  33.4 1.5 convolution_bitcast_fusion
  35.6 7.5 %all_gather.30 = bf16[1024,1,128]{0,2,1:T(8,128)(2,1)} all-gather(bf16[512,1,128]{0,2,1:T(8,128)(2,1)S(1)} %pad_maximum_fusion.1), channel_id=1, replica_groups=mesh['ctx_0'=2,'ctx_1'=4,'ctx_2'=2,'tp'=8] {'ctx_0'}, dimensions={0}, use_global_device_ids=true | all-gather | bytes 393216 | tf_op jit(solution)/shard_map/all_gather | solution.py:15
  43.2 3.4 convolution_convert_fusion.1
  46.6 7.2 %all-gather = bf16[1024,128]{1,0:T(8,128)(2,1)} all-gather(bf16[512,128]{1,0:T(8,128)(2,1)S(1)} %convolution_convert_fusion.1), channel_id=2, replica_groups=mesh['ctx_0'=2,'ctx_1'=4,'ctx_2'=2,'tp'=8] {'ctx_0'}, dimensions={0}, use_global_device_ids=true | all-gather | bytes 393216 | tf_op jit(solution)/shard_map/all_gather | solution.py:15
  53.9 13.6 %all-gather.9.cloned.1.call-done = bf16[4096,1,128]{0,2,1:T(8,128)(2,1)} async-done(((bf16[1024,1,128]{0,2,1:T(8,128)(2,1)}), bf16[4096,1,128]{0,2,1:T(8,128)(2,1)}) %all-gather.9.cloned.1.call-update) | async-done | bytes 1048592 | tf_op jit(solution)/shard_map/all_gather | solution.py:15
  67.8 25.9 %all-gather.13.cloned.1.call-done = bf16[4096,128]{1,0:T(8,128)(2,1)} async-done(((bf16[1024,128]{1,0:T(8,128)(2,1)}), bf16[4096,128]{1,0:T(8,128)(2,1)}) %all-gather.13.cloned.1.call-update) | async-done | bytes 1048592 | tf_op jit(solution)/shard_map/all_gather | solution.py:15
  93.7 5.8 %fusion.49 = f32[512,512]{0,1:T(8,128)S(1)} fusion(bf16[512,4096]{1,0:T(8,128)(2,1)} %copy-done.5, bf16[4096,512]{1,0:T(8,128)(2,1)} %param.17), kind=kOutput, calls=%fused_computation.90 | convolution fusion | flops 2147483648 | bytes 9437184 | tf_op jit(solution)/shard_map/dot_general | solution.py:118
  100.3 5.9 %all-gather.3 = s32[2,1,512]{2,1,0:T(1,128)S(1)} all-gather(s32[1,1,512]{2,1,0:T(1,128)S(1)} %bitcast.138), channel_id=1, replica_groups=mesh['ctx_0'=2,'ctx_1'=4,'ctx_2'=2,'tp'=8] {'ctx_0'}, dimensions={0}, use_global_device_ids=true | all-gather | bytes 6144 | tf_op jit(solution)/shard_map/all_gather | solution.py:15
  106.2 12.0 %all_gather.28 = s32[4096]{0:T(1024)S(1)} all-gather(s32[1024]{0:T(1024)S(1)} %bitcast.137), channel_id=1, replica_groups=mesh['ctx_0'=2,'ctx_1'=4,'ctx_2'=2,'tp'=8] {'ctx_1'}, dimensions={0}, use_global_device_ids=true | all-gather | bytes 20480 | tf_op jit(solution)/shard_map/all_gather | solution.py:15
  118.2 1.8 all_gather.29
  123.5 2.9 all-gather.15.cloned.1.call-done
  126.4 172.4 %conditional.1 = (f32[1,4,512]{2,1,0:T(4,128)}, f32[1,4,512,128]{2,3,1,0:T(8,128)S(1)}) conditional(s32[]{:T(128)} %convert_element_type.59, () %tuple.21, (bf16[8192,1,128]{0,2,1:T(8,128)(2,1)}, bf16[8192,1,128]{2,0,1:T(8,128)(2,1)}, s32[8192]{0:T(1024)S(1)}, s32[512]{0:T(512)S(1)}, bf16[512,1,4,128]{3,0,2,1:T(8,128)(2,1)S(1)}) %tuple.72), branch_computations={%region_3.4_spmd, %region_4.9_spmd} | conditional | flops 551563264 | bytes 39789324 | solution.py:91
  126.4 3.2 copy.22
  129.7 167.6 %while.15 = (s32[]{:T(128)}, f32[1,4,512]{2,1,0:T(4,128)S(1)}, f32[1,4,512]{2,1,0:T(4,128)}, f32[1,4,512,128]{3,2,1,0:T(8,128)}, s32[16,512]{1,0:T(8,128)S(1)}, ...) while((s32[]{:T(128)}, f32[1,4,512]{2,1,0:T(4,128)S(1)}, ...), condition=%wide.region_8.8_spmd.clone, body=%wide.region_5.7_spmd.clone.sunk | while | flops 551563264 | bytes 33432220 | solution.py:85
  129.9 2.8 fusion.66
  132.8 4.8 %fusion.69 = f32[1,4,512,128]{3,2,1,0:T(8,128)} fusion(f32[512,512,4]{1,0,2:T(8,128)} %get-tuple-element.232, f32[4,512]{1,0:T(4,128)S(1)} %bitcast.132, pred[512,512]{0,1:T(8,128)(4,1)S(1)} %broadcast_compare_fusion.2, f32[1,4,512,128]{3,2,1,0:T(8,128)} %get-tuple-element.248, f32[4,512]{1,0:T(4,128)S(1)} %get-tuple-element.233, pred[]{:T(512)S(6)} %compare.27, ...), kind=kOutput, calls=%fused_computation.12.clone.1 | convolution fusion | flops 274464768 | bytes 6701569 | tf_op jit(solution)/shard_map/cond/branch_1_fun/while/body/eval_jaxpr/kgqn,nkd->kgqd/dot_general | solution.py:63
  139.5 2.8 fusion.66
  142.3 5.1 %fusion.69 = f32[1,4,512,128]{3,2,1,0:T(8,128)} fusion(f32[512,512,4]{1,0,2:T(8,128)} %get-tuple-element.232, f32[4,512]{1,0:T(4,128)S(1)} %bitcast.132, pred[512,512]{0,1:T(8,128)(4,1)S(1)} %broadcast_compare_fusion.2, f32[1,4,512,128]{3,2,1,0:T(8,128)} %get-tuple-element.248, f32[4,512]{1,0:T(4,128)S(1)} %get-tuple-element.233, pred[]{:T(512)S(6)} %compare.27, ...), kind=kOutput, calls=%fused_computation.12.clone.1 | convolution fusion | flops 274464768 | bytes 6701569 | tf_op jit(solution)/shard_map/cond/branch_1_fun/while/body/eval_jaxpr/kgqn,nkd->kgqd/dot_general | solution.py:63
  150.0 2.8 fusion.66
  152.8 5.1 %fusion.69 = f32[1,4,512,128]{3,2,1,0:T(8,128)} fusion(f32[512,512,4]{1,0,2:T(8,128)} %get-tuple-element.232, f32[4,512]{1,0:T(4,128)S(1)} %bitcast.132, pred[512,512]{0,1:T(8,128)(4,1)S(1)} %broadcast_compare_fusion.2, f32[1,4,512,128]{3,2,1,0:T(8,128)} %get-tuple-element.248, f32[4,512]{1,0:T(4,128)S(1)} %get-tuple-element.233, pred[]{:T(512)S(6)} %compare.27, ...), kind=kOutput, calls=%fused_computation.12.clone.1 | convolution fusion | flops 274464768 | bytes 6701569 | tf_op jit(solution)/shard_map/cond/branch_1_fun/while/body/eval_jaxpr/kgqn,nkd->kgqd/dot_general | solution.py:63
  160.5 2.8 fusion.66
  163.4 5.1 %fusion.69 = f32[1,4,512,128]{3,2,1,0:T(8,128)} fusion(f32[512,512,4]{1,0,2:T(8,128)} %get-tuple-element.232, f32[4,512]{1,0:T(4,128)S(1)} %bitcast.132, pred[512,512]{0,1:T(8,128)(4,1)S(1)} %broadcast_compare_fusion.2, f32[1,4,512,128]{3,2,1,0:T(8,128)} %get-tuple-element.248, f32[4,512]{1,0:T(4,128)S(1)} %get-tuple-element.233, pred[]{:T(512)S(6)} %compare.27, ...), kind=kOutput, calls=%fused_computation.12.clone.1 | convolution fusion | flops 274464768 | bytes 6701569 | tf_op jit(solution)/shard_map/cond/branch_1_fun/while/body/eval_jaxpr/kgqn,nkd->kgqd/dot_general | solution.py:63
  169.5 1.3 bitcast_add_fusion.2
  171.1 2.8 fusion.66
  173.9 5.1 %fusion.69 = f32[1,4,512,128]{3,2,1,0:T(8,128)} fusion(f32[512,512,4]{1,0,2:T(8,128)} %get-tuple-element.232, f32[4,512]{1,0:T(4,128)S(1)} %bitcast.132, pred[512,512]{0,1:T(8,128)(4,1)S(1)} %broadcast_compare_fusion.2, f32[1,4,512,128]{3,2,1,0:T(8,128)} %get-tuple-element.248, f32[4,512]{1,0:T(4,128)S(1)} %get-tuple-element.233, pred[]{:T(512)S(6)} %compare.27, ...), kind=kOutput, calls=%fused_computation.12.clone.1 | convolution fusion | flops 274464768 | bytes 6701569 | tf_op jit(solution)/shard_map/cond/branch_1_fun/while/body/eval_jaxpr/kgqn,nkd->kgqd/dot_general | solution.py:63
  181.6 2.8 fusion.66
  184.4 5.1 %fusion.69 = f32[1,4,512,128]{3,2,1,0:T(8,128)} fusion(f32[512,512,4]{1,0,2:T(8,128)} %get-tuple-element.232, f32[4,512]{1,0:T(4,128)S(1)} %bitcast.132, pred[512,512]{0,1:T(8,128)(4,1)S(1)} %broadcast_compare_fusion.2, f32[1,4,512,128]{3,2,1,0:T(8,128)} %get-tuple-element.248, f32[4,512]{1,0:T(4,128)S(1)} %get-tuple-element.233, pred[]{:T(512)S(6)} %compare.27, ...), kind=kOutput, calls=%fused_computation.12.clone.1 | convolution fusion | flops 274464768 | bytes 6701569 | tf_op jit(solution)/shard_map/cond/branch_1_fun/while/body/eval_jaxpr/kgqn,nkd->kgqd/dot_general | solution.py:63
  192.1 2.8 fusion.66
  195.0 5.1 %fusion.69 = f32[1,4,512,128]{3,2,1,0:T(8,128)} fusion(f32[512,512,4]{1,0,2:T(8,128)} %get-tuple-element.232, f32[4,512]{1,0:T(4,128)S(1)} %bitcast.132, pred[512,512]{0,1:T(8,128)(4,1)S(1)} %broadcast_compare_fusion.2, f32[1,4,512,128]{3,2,1,0:T(8,128)} %get-tuple-element.248, f32[4,512]{1,0:T(4,128)S(1)} %get-tuple-element.233, pred[]{:T(512)S(6)} %compare.27, ...), kind=kOutput, calls=%fused_computation.12.clone.1 | convolution fusion | flops 274464768 | bytes 6701569 | tf_op jit(solution)/shard_map/cond/branch_1_fun/while/body/eval_jaxpr/kgqn,nkd->kgqd/dot_general | solution.py:63
  202.7 2.8 fusion.66
  205.5 5.1 %fusion.69 = f32[1,4,512,128]{3,2,1,0:T(8,128)} fusion(f32[512,512,4]{1,0,2:T(8,128)} %get-tuple-element.232, f32[4,512]{1,0:T(4,128)S(1)} %bitcast.132, pred[512,512]{0,1:T(8,128)(4,1)S(1)} %broadcast_compare_fusion.2, f32[1,4,512,128]{3,2,1,0:T(8,128)} %get-tuple-element.248, f32[4,512]{1,0:T(4,128)S(1)} %get-tuple-element.233, pred[]{:T(512)S(6)} %compare.27, ...), kind=kOutput, calls=%fused_computation.12.clone.1 | convolution fusion | flops 274464768 | bytes 6701569 | tf_op jit(solution)/shard_map/cond/branch_1_fun/while/body/eval_jaxpr/kgqn,nkd->kgqd/dot_general | solution.py:63
  213.2 2.8 fusion.66
  216.0 5.1 %fusion.69 = f32[1,4,512,128]{3,2,1,0:T(8,128)} fusion(f32[512,512,4]{1,0,2:T(8,128)} %get-tuple-element.232, f32[4,512]{1,0:T(4,128)S(1)} %bitcast.132, pred[512,512]{0,1:T(8,128)(4,1)S(1)} %broadcast_compare_fusion.2, f32[1,4,512,128]{3,2,1,0:T(8,128)} %get-tuple-element.248, f32[4,512]{1,0:T(4,128)S(1)} %get-tuple-element.233, pred[]{:T(512)S(6)} %compare.27, ...), kind=kOutput, calls=%fused_computation.12.clone.1 | convolution fusion | flops 274464768 | bytes 6701569 | tf_op jit(solution)/shard_map/cond/branch_1_fun/while/body/eval_jaxpr/kgqn,nkd->kgqd/dot_general | solution.py:63
  223.7 2.8 fusion.66
  226.6 5.1 %fusion.69 = f32[1,4,512,128]{3,2,1,0:T(8,128)} fusion(f32[512,512,4]{1,0,2:T(8,128)} %get-tuple-element.232, f32[4,512]{1,0:T(4,128)S(1)} %bitcast.132, pred[512,512]{0,1:T(8,128)(4,1)S(1)} %broadcast_compare_fusion.2, f32[1,4,512,128]{3,2,1,0:T(8,128)} %get-tuple-element.248, f32[4,512]{1,0:T(4,128)S(1)} %get-tuple-element.233, pred[]{:T(512)S(6)} %compare.27, ...), kind=kOutput, calls=%fused_computation.12.clone.1 | convolution fusion | flops 274464768 | bytes 6701569 | tf_op jit(solution)/shard_map/cond/branch_1_fun/while/body/eval_jaxpr/kgqn,nkd->kgqd/dot_general | solution.py:63
  232.7 1.3 bitcast_add_fusion.2
  234.3 2.8 fusion.66
  237.1 5.1 %fusion.69 = f32[1,4,512,128]{3,2,1,0:T(8,128)} fusion(f32[512,512,4]{1,0,2:T(8,128)} %get-tuple-element.232, f32[4,512]{1,0:T(4,128)S(1)} %bitcast.132, pred[512,512]{0,1:T(8,128)(4,1)S(1)} %broadcast_compare_fusion.2, f32[1,4,512,128]{3,2,1,0:T(8,128)} %get-tuple-element.248, f32[4,512]{1,0:T(4,128)S(1)} %get-tuple-element.233, pred[]{:T(512)S(6)} %compare.27, ...), kind=kOutput, calls=%fused_computation.12.clone.1 | convolution fusion | flops 274464768 | bytes 6701569 | tf_op jit(solution)/shard_map/cond/branch_1_fun/while/body/eval_jaxpr/kgqn,nkd->kgqd/dot_general | solution.py:63
  244.8 2.8 fusion.66
  247.6 5.1 %fusion.69 = f32[1,4,512,128]{3,2,1,0:T(8,128)} fusion(f32[512,512,4]{1,0,2:T(8,128)} %get-tuple-element.232, f32[4,512]{1,0:T(4,128)S(1)} %bitcast.132, pred[512,512]{0,1:T(8,128)(4,1)S(1)} %broadcast_compare_fusion.2, f32[1,4,512,128]{3,2,1,0:T(8,128)} %get-tuple-element.248, f32[4,512]{1,0:T(4,128)S(1)} %get-tuple-element.233, pred[]{:T(512)S(6)} %compare.27, ...), kind=kOutput, calls=%fused_computation.12.clone.1 | convolution fusion | flops 274464768 | bytes 6701569 | tf_op jit(solution)/shard_map/cond/branch_1_fun/while/body/eval_jaxpr/kgqn,nkd->kgqd/dot_general | solution.py:63
  255.3 2.8 fusion.66
  258.2 5.1 %fusion.69 = f32[1,4,512,128]{3,2,1,0:T(8,128)} fusion(f32[512,512,4]{1,0,2:T(8,128)} %get-tuple-element.232, f32[4,512]{1,0:T(4,128)S(1)} %bitcast.132, pred[512,512]{0,1:T(8,128)(4,1)S(1)} %broadcast_compare_fusion.2, f32[1,4,512,128]{3,2,1,0:T(8,128)} %get-tuple-element.248, f32[4,512]{1,0:T(4,128)S(1)} %get-tuple-element.233, pred[]{:T(512)S(6)} %compare.27, ...), kind=kOutput, calls=%fused_computation.12.clone.1 | convolution fusion | flops 274464768 | bytes 6701569 | tf_op jit(solution)/shard_map/cond/branch_1_fun/while/body/eval_jaxpr/kgqn,nkd->kgqd/dot_general | solution.py:63
  265.9 2.8 fusion.66
  268.7 5.1 %fusion.69 = f32[1,4,512,128]{3,2,1,0:T(8,128)} fusion(f32[512,512,4]{1,0,2:T(8,128)} %get-tuple-element.232, f32[4,512]{1,0:T(4,128)S(1)} %bitcast.132, pred[512,512]{0,1:T(8,128)(4,1)S(1)} %broadcast_compare_fusion.2, f32[1,4,512,128]{3,2,1,0:T(8,128)} %get-tuple-element.248, f32[4,512]{1,0:T(4,128)S(1)} %get-tuple-element.233, pred[]{:T(512)S(6)} %compare.27, ...), kind=kOutput, calls=%fused_computation.12.clone.1 | convolution fusion | flops 274464768 | bytes 6701569 | tf_op jit(solution)/shard_map/cond/branch_1_fun/while/body/eval_jaxpr/kgqn,nkd->kgqd/dot_general | solution.py:63
  276.4 2.8 fusion.66
  279.2 5.1 %fusion.69 = f32[1,4,512,128]{3,2,1,0:T(8,128)} fusion(f32[512,512,4]{1,0,2:T(8,128)} %get-tuple-element.232, f32[4,512]{1,0:T(4,128)S(1)} %bitcast.132, pred[512,512]{0,1:T(8,128)(4,1)S(1)} %broadcast_compare_fusion.2, f32[1,4,512,128]{3,2,1,0:T(8,128)} %get-tuple-element.248, f32[4,512]{1,0:T(4,128)S(1)} %get-tuple-element.233, pred[]{:T(512)S(6)} %compare.27, ...), kind=kOutput, calls=%fused_computation.12.clone.1 | convolution fusion | flops 274464768 | bytes 6701569 | tf_op jit(solution)/shard_map/cond/branch_1_fun/while/body/eval_jaxpr/kgqn,nkd->kgqd/dot_general | solution.py:63
  286.9 2.8 fusion.66
  289.8 5.1 %fusion.69 = f32[1,4,512,128]{3,2,1,0:T(8,128)} fusion(f32[512,512,4]{1,0,2:T(8,128)} %get-tuple-element.232, f32[4,512]{1,0:T(4,128)S(1)} %bitcast.132, pred[512,512]{0,1:T(8,128)(4,1)S(1)} %broadcast_compare_fusion.2, f32[1,4,512,128]{3,2,1,0:T(8,128)} %get-tuple-element.248, f32[4,512]{1,0:T(4,128)S(1)} %get-tuple-element.233, pred[]{:T(512)S(6)} %compare.27, ...), kind=kOutput, calls=%fused_computation.12.clone.1 | convolution fusion | flops 274464768 | bytes 6701569 | tf_op jit(solution)/shard_map/cond/branch_1_fun/while/body/eval_jaxpr/kgqn,nkd->kgqd/dot_general | solution.py:63
  297.3 1.6 copy.27
  299.7 4.6 %convolution_convert_fusion = bf16[512,4096]{1,0:T(8,128)(2,1)S(1)} fusion(bf16[512,512]{0,1:T(8,128)(2,1)S(1)} %bitcast.134, bf16[512,4096]{1,0:T(8,128)(2,1)} %param.20), kind=kOutput, calls=%fused_computation.36 | convolution fusion | flops 2149580800 | bytes 8912896 | tf_op jit(solution)/shard_map/dot_general | solution.py:133
  304.2 2.4 copy.32
  306.6 5.1 %all-to-all-start = ((bf16[8,512,512]{2,1,0:T(8,128)(2,1)}), bf16[8,512,512]{2,1,0:T(8,128)(2,1)}, u32[]{:S(2)}, u32[]{:S(2)}) async-start(bf16[8,512,512]{2,1,0:T(8,128)(2,1)} %bitcast.129), calls=%async_computation | async-start | bytes 8388608 | tf_op jit(solution)/shard_map/all_to_all | solution.py:27
  311.7 2.3 gather_fusion
  314.0 1.5 dynamic-slice_convert_fusion
  315.5 56.3 %all-to-all-done = bf16[8,512,512]{2,1,0:T(8,128)(2,1)} async-done(((bf16[8,512,512]{2,1,0:T(8,128)(2,1)}), bf16[8,512,512]{2,1,0:T(8,128)(2,1)}, u32[]{:S(2)}, u32[]{:S(2)}) %all-to-all-start) | async-done | bytes 4194336 | tf_op jit(solution)/shard_map/all_to_all | solution.py:27
  371.8 3.9 %convert_reduce_fusion = f32[512,512]{1,0:T(8,128)} fusion(bf16[8,512,512]{2,1,0:T(8,128)(2,1)} %all-to-all-done), kind=kLoop, calls=%fused_computation.32 | loop fusion | flops 3932160 | bytes 5242880 | tf_op jit(solution)/shard_map/reduce_sum | solution.py:28
  375.7 5.2 %scatter_custom_fusion = f32[1024,512]{1,0:T(8,128)S(1)} fusion(f32[1024,512]{1,0:T(8,128)S(1)} %dynamic-slice_convert_fusion, s32[512]{0:T(512)S(1)} %get-tuple-element.166, f32[512,512]{1,0:T(8,128)} %convert_reduce_fusion, f32[512]{0:T(512)S(1)} %gather_fusion), kind=kCustom, calls=%fused_computation.40 | custom fusion | flops 524288 | bytes 3147776 | tf_op jit(solution)/shard_map/scatter-add | solution.py:141
  (171 shorter events, 44.9 us)
Async XLA Ops:
  6.5 26.9 %copy-start = (bf16[4096,128]{1,0:T(8,128)(2,1)S(1)}, bf16[4096,128]{1,0:T(8,128)(2,1)}, u32[]{:S(2)}) copy-start(bf16[4096,128]{1,0:T(8,128)(2,1)} %param.18) | copy-start | bytes 3145732
  6.5 61.0 %all-gather.9.cloned.1.call-start = ((), (), s32[]{:S(2)}) async-start(), calls=%async_computation.1 | async-start | bytes 1310720 | tf_op jit(solution)/shard_map/all_gather | solution.py:15
  12.5 16.6 %copy-start.6 = (f32[4096]{0:T(1024)S(1)}, f32[4096]{0:T(1024)}, u32[]{:S(2)}) copy-start(f32[4096]{0:T(1024)} %param.16) | copy-start | bytes 49156
  25.6 3.6 copy-start.4
  31.5 1.9 copy-start.5
  33.4 9.7 %copy-start.7 = (bf16[4096,128]{1,0:T(8,128)(2,1)S(1)}, bf16[4096,128]{1,0:T(8,128)(2,1)}, u32[]{:S(2)}) copy-start(bf16[4096,128]{1,0:T(8,128)(2,1)} %param.19) | copy-start | bytes 3145732
  43.1 50.6 %all-gather.13.cloned.1.call-start = ((), (), s32[]{:S(2)}) async-start(), calls=%async_computation.3 | async-start | bytes 1310720 | tf_op jit(solution)/shard_map/all_gather | solution.py:15
  53.9 69.6 %all-gather.11.cloned.1.call-start = ((), (), s32[]{:S(2)}) async-start(), calls=%async_computation.2 | async-start | bytes 3145728 | tf_op jit(solution)/shard_map/all_gather | solution.py:15
  67.6 58.9 %all-gather.15.cloned.1.call-start = ((), (), s32[]{:S(2)}) async-start(), calls=%async_computation.4 | async-start | bytes 3145728 | tf_op jit(solution)/shard_map/all_gather | solution.py:15
  132.8 4.8 %copy-start.3 = (f32[512,512,4]{1,0,2:T(8,128)S(1)}, f32[512,512,4]{1,0,2:T(8,128)}, u32[]{:S(2)}) copy-start(f32[512,512,4]{1,0,2:T(8,128)} %get-tuple-element.232) | copy-start | bytes 12582916 | tf_op jit(solution)/shard_map/cond/branch_1_fun/while
  142.3 5.1 %copy-start.3 = (f32[512,512,4]{1,0,2:T(8,128)S(1)}, f32[512,512,4]{1,0,2:T(8,128)}, u32[]{:S(2)}) copy-start(f32[512,512,4]{1,0,2:T(8,128)} %get-tuple-element.232) | copy-start | bytes 12582916 | tf_op jit(solution)/shard_map/cond/branch_1_fun/while
  152.8 5.1 %copy-start.3 = (f32[512,512,4]{1,0,2:T(8,128)S(1)}, f32[512,512,4]{1,0,2:T(8,128)}, u32[]{:S(2)}) copy-start(f32[512,512,4]{1,0,2:T(8,128)} %get-tuple-element.232) | copy-start | bytes 12582916 | tf_op jit(solution)/shard_map/cond/branch_1_fun/while
  163.4 5.1 %copy-start.3 = (f32[512,512,4]{1,0,2:T(8,128)S(1)}, f32[512,512,4]{1,0,2:T(8,128)}, u32[]{:S(2)}) copy-start(f32[512,512,4]{1,0,2:T(8,128)} %get-tuple-element.232) | copy-start | bytes 12582916 | tf_op jit(solution)/shard_map/cond/branch_1_fun/while
  173.9 5.1 %copy-start.3 = (f32[512,512,4]{1,0,2:T(8,128)S(1)}, f32[512,512,4]{1,0,2:T(8,128)}, u32[]{:S(2)}) copy-start(f32[512,512,4]{1,0,2:T(8,128)} %get-tuple-element.232) | copy-start | bytes 12582916 | tf_op jit(solution)/shard_map/cond/branch_1_fun/while
  184.4 5.1 %copy-start.3 = (f32[512,512,4]{1,0,2:T(8,128)S(1)}, f32[512,512,4]{1,0,2:T(8,128)}, u32[]{:S(2)}) copy-start(f32[512,512,4]{1,0,2:T(8,128)} %get-tuple-element.232) | copy-start | bytes 12582916 | tf_op jit(solution)/shard_map/cond/branch_1_fun/while
  195.0 5.1 %copy-start.3 = (f32[512,512,4]{1,0,2:T(8,128)S(1)}, f32[512,512,4]{1,0,2:T(8,128)}, u32[]{:S(2)}) copy-start(f32[512,512,4]{1,0,2:T(8,128)} %get-tuple-element.232) | copy-start | bytes 12582916 | tf_op jit(solution)/shard_map/cond/branch_1_fun/while
  205.5 5.1 %copy-start.3 = (f32[512,512,4]{1,0,2:T(8,128)S(1)}, f32[512,512,4]{1,0,2:T(8,128)}, u32[]{:S(2)}) copy-start(f32[512,512,4]{1,0,2:T(8,128)} %get-tuple-element.232) | copy-start | bytes 12582916 | tf_op jit(solution)/shard_map/cond/branch_1_fun/while
  216.0 5.1 %copy-start.3 = (f32[512,512,4]{1,0,2:T(8,128)S(1)}, f32[512,512,4]{1,0,2:T(8,128)}, u32[]{:S(2)}) copy-start(f32[512,512,4]{1,0,2:T(8,128)} %get-tuple-element.232) | copy-start | bytes 12582916 | tf_op jit(solution)/shard_map/cond/branch_1_fun/while
  226.6 5.1 %copy-start.3 = (f32[512,512,4]{1,0,2:T(8,128)S(1)}, f32[512,512,4]{1,0,2:T(8,128)}, u32[]{:S(2)}) copy-start(f32[512,512,4]{1,0,2:T(8,128)} %get-tuple-element.232) | copy-start | bytes 12582916 | tf_op jit(solution)/shard_map/cond/branch_1_fun/while
  237.1 5.1 %copy-start.3 = (f32[512,512,4]{1,0,2:T(8,128)S(1)}, f32[512,512,4]{1,0,2:T(8,128)}, u32[]{:S(2)}) copy-start(f32[512,512,4]{1,0,2:T(8,128)} %get-tuple-element.232) | copy-start | bytes 12582916 | tf_op jit(solution)/shard_map/cond/branch_1_fun/while
  247.6 5.1 %copy-start.3 = (f32[512,512,4]{1,0,2:T(8,128)S(1)}, f32[512,512,4]{1,0,2:T(8,128)}, u32[]{:S(2)}) copy-start(f32[512,512,4]{1,0,2:T(8,128)} %get-tuple-element.232) | copy-start | bytes 12582916 | tf_op jit(solution)/shard_map/cond/branch_1_fun/while
  258.2 5.1 %copy-start.3 = (f32[512,512,4]{1,0,2:T(8,128)S(1)}, f32[512,512,4]{1,0,2:T(8,128)}, u32[]{:S(2)}) copy-start(f32[512,512,4]{1,0,2:T(8,128)} %get-tuple-element.232) | copy-start | bytes 12582916 | tf_op jit(solution)/shard_map/cond/branch_1_fun/while
  268.7 5.1 %copy-start.3 = (f32[512,512,4]{1,0,2:T(8,128)S(1)}, f32[512,512,4]{1,0,2:T(8,128)}, u32[]{:S(2)}) copy-start(f32[512,512,4]{1,0,2:T(8,128)} %get-tuple-element.232) | copy-start | bytes 12582916 | tf_op jit(solution)/shard_map/cond/branch_1_fun/while
  279.2 5.1 %copy-start.3 = (f32[512,512,4]{1,0,2:T(8,128)S(1)}, f32[512,512,4]{1,0,2:T(8,128)}, u32[]{:S(2)}) copy-start(f32[512,512,4]{1,0,2:T(8,128)} %get-tuple-element.232) | copy-start | bytes 12582916 | tf_op jit(solution)/shard_map/cond/branch_1_fun/while
  289.8 5.1 %copy-start.3 = (f32[512,512,4]{1,0,2:T(8,128)S(1)}, f32[512,512,4]{1,0,2:T(8,128)}, u32[]{:S(2)}) copy-start(f32[512,512,4]{1,0,2:T(8,128)} %get-tuple-element.232) | copy-start | bytes 12582916 | tf_op jit(solution)/shard_map/cond/branch_1_fun/while
  306.6 5.1 %copy-start.2 = (f32[1024]{0:T(1024)S(1)}, f32[1024]{0:T(1024)}, u32[]{:S(2)}) copy-start(f32[1024]{0:T(1024)} %param.23) | copy-start | bytes 12292
  306.6 65.2 %all-to-all-start = ((bf16[8,512,512]{2,1,0:T(8,128)(2,1)}), bf16[8,512,512]{2,1,0:T(8,128)(2,1)}, u32[]{:S(2)}, u32[]{:S(2)}) async-start(bf16[8,512,512]{2,1,0:T(8,128)(2,1)} %bitcast.129), calls=%async_computation | async-start | bytes 8388608 | tf_op jit(solution)/shard_map/all_to_all | solution.py:27
  371.8 10.2 %copy-start.1 = (bf16[4096,128]{1,0:T(8,128)(2,1)S(1)}, bf16[4096,128]{1,0:T(8,128)(2,1)}, u32[]{:S(2)}) copy-start(bf16[4096,128]{1,0:T(8,128)(2,1)} %param.18) | copy-start | bytes 3145732
Sparse Core Ops, SparseCore 0:
  43.2 24.2 all-gather.8
  69.2 24.4 all-gather.12
  95.3 14.8 all-gather.10
  111.8 14.6 all-gather.14
where the time goes:
time: 391 us; the launch traced here: 389 us
  matrix products  142 us (36%)
  waiting for transfers between devices  98.8 us (25%)
  other arithmetic  66.4 us (17%)
  blocking collectives  34.5 us (9%)
  local copies, waits for them, and re-layouts  26.9 us (7%)
  between operations  14.6 us (4%)
  starting transfers between devices  5.38 us (1%)
    dot_general x16, matrix products, block_step(): jnp.einsum('kgqn,nkd->kgqd', weight.astype(jnp.bfloat16), block_values, p...  81.3 us
    all_to_all x1, waiting for transfers between devices, sent_and_summed(): lax.all_to_all(parts, axis, split_axis=0, concat_axis=0, tiled=True)  56.3 us
    dot_general x16, matrix products, block_step(): jnp.einsum('qkgd,nkd->kgqn', queries, block_keys, preferred_element_type=...  44.9 us
    all_gather x4, waiting for transfers between devices, gathered_by_axis(): nearer = lax.all_gather(value, axes[-1], axis=dim, tiled=True)  42.4 us
    all_gather x5, blocking collectives, gathered_by_axis(): nearer = lax.all_gather(value, axes[-1], axis=dim, tiled=True)  34.5 us
    add x16, other arithmetic, block_step(): total = total * factor + jnp.sum(weight, axis=-1)  20.3 us
    reduce_sum x16, other arithmetic, block_step(): total = total * factor + jnp.sum(weight, axis=-1)  16.7 us
    gather x1, local copies, waits for them, and re-layouts, per_device(): rows = hidden[index].astype(jnp.float32) * live[:, None].astype(jnp.float32)  13 us
  transfers between devices with their start and end apart: 5, of which 4 were waited for; matrix products, arithmetic and copies ran while one was open for 4% of the time, Pallas kernels for 0%

commit v1 on v0

v1 whole, which is shorter than its diff:
```python
import functools

import jax
import jax.numpy as jnp
import numpy as np
from jax import lax
from jax.experimental import pallas as pl
from jax.experimental.pallas import tpu as pltpu
from jax.sharding import Mesh
from jax.sharding import PartitionSpec as P

HEAD_DIM = 128
BLOCK = 128
CTX = ("zh", "y", "core")
TP = ("x", "zl")
CHUNK = 512
KEY_CHUNK = 512
STEP = 32
F32 = jnp.float32
BF16 = jnp.bfloat16
VMEM_LIMIT = 60 * 1024 * 1024


def freq_table():
    half = HEAD_DIM // 2
    one = 500000.0 ** (-2.0 * np.arange(half, dtype=np.float64) / HEAD_DIM)
    return np.concatenate([one, one])


def angle_tables(seq, shards):
    freq = freq_table()
    sign = np.concatenate([-np.ones(HEAD_DIM // 2), np.ones(HEAD_DIM // 2)])
    coarse = np.arange(0, seq * shards, STEP, dtype=np.float64)[:, None] * freq[None, :]
    fine = np.arange(STEP, dtype=np.float64)[:, None] * freq[None, :]
    big = np.stack([np.cos(coarse), np.sin(coarse)]).astype(np.float32)
    small = np.stack([np.cos(fine), np.sin(fine), np.tile(sign, (STEP, 1))]).astype(np.float32)
    return big.reshape(2, shards, seq // STEP, HEAD_DIM).transpose(1, 0, 2, 3), small


def live_rows(counts_ref, blocks):
    total = counts_ref[0]
    for block in range(1, blocks):
        total = total + counts_ref[block]
    return total


def compact_positions(counts_ref, pos_ref, base, slots):
    lane = lax.broadcasted_iota(jnp.int32, (1, BLOCK), 1)
    row = lax.broadcasted_iota(jnp.int32, (slots, BLOCK), 0)
    start = jnp.int32(0)
    total = jnp.zeros((slots, BLOCK), F32)
    for block in range(slots // BLOCK):
        count = counts_ref[block]
        place = jnp.where(lane < count, lane + start, -1)
        value = (pos_ref[:, block * BLOCK : (block + 1) * BLOCK] - (base - 1)).astype(F32)
        total = total + jnp.where(place == row, value, 0.0)
        start = start + count
    return jnp.sum(total, axis=1, keepdims=True).astype(jnp.int32) - 1


def select_matrix(counts_ref, pos_ref, base, slots, seq):
    column = compact_positions(counts_ref, pos_ref, base, slots)
    place = lax.broadcasted_iota(jnp.int32, (slots, seq), 1)
    return jnp.where(place == column, 1.0, 0.0).astype(BF16)


def rotated(field, cos, sin):
    return field * cos + pltpu.roll(field, HEAD_DIM // 2, 1) * sin


def front_kernel(
    shard_ref, counts_ref, pos_ref, gain_ref, big_ref, small_ref, hidden, wq, wk, wv,
    q_out, kv_out,
    hbuf, wkv, wqv, xg, acc_kv, acc_q, ssq, cos, sin, sel, hsem, wsem,
):
    seq, width = hidden.shape
    slots = pos_ref.shape[1]
    chunks = width // CHUNK
    rows = 256
    blocks = seq // rows
    copies_w = [
        pltpu.make_async_copy(wk, wkv.at[:, :HEAD_DIM], wsem.at[0]),
        pltpu.make_async_copy(wv, wkv.at[:, HEAD_DIM:], wsem.at[1]),
        pltpu.make_async_copy(wq, wqv, wsem.at[2]),
    ]

    def fetch(chunk):
        columns = pl.ds(pl.multiple_of(chunk * CHUNK, CHUNK), CHUNK)
        slot = lax.rem(chunk, 3)
        return pltpu.make_async_copy(hidden.at[:, columns], hbuf.at[slot], hsem.at[slot])

    copies_w[0].start()
    copies_w[1].start()
    fetch(0).start()
    fetch(1).start()
    copies_w[2].start()

    base = shard_ref[0] * seq
    for step in range(seq // STEP):
        part = slice(step * STEP, (step + 1) * STEP)
        cb, sb = big_ref[0, step : step + 1, :], big_ref[1, step : step + 1, :]
        cf, sf, sign = small_ref[0], small_ref[1], small_ref[2]
        cos[part, :] = cb * cf - sb * sf
        sin[part, :] = (sb * cf + cb * sf) * sign
    sel[...] = select_matrix(counts_ref, pos_ref, base, slots, seq)
    acc_kv[...] = jnp.zeros_like(acc_kv)
    ssq[...] = jnp.zeros_like(ssq)
    copies_w[0].wait()
    copies_w[1].wait()

    @pl.loop(0, chunks)
    def _(chunk):
        fetch(chunk).wait()

        @pl.when(chunk + 2 < chunks)
        def _():
            fetch(chunk + 2).start()

        slot = lax.rem(chunk, 3)
        columns = pl.ds(pl.multiple_of(chunk * CHUNK, CHUNK), CHUNK)
        gain = gain_ref[:, columns]
        weight = wkv[columns, :]
        for block in range(blocks):
            part = slice(block * rows, (block + 1) * rows)
            value = hbuf[slot, part, :].astype(F32)
            square = value * value
            partial = square[:, :128]
            for lane in range(1, CHUNK // 128):
                partial = partial + square[:, lane * 128 : (lane + 1) * 128]
            ssq[part, :] += partial
            scaled = (value * gain).astype(BF16)
            xg[part, columns] = scaled
            acc_kv[part, :] += jnp.dot(scaled, weight, preferred_element_type=F32)

    def scale_of(part):
        mean = jnp.sum(ssq[part, :], axis=1, keepdims=True) * (1.0 / width)
        return lax.rsqrt(mean + 1e-05)

    pieces = []
    for block in range(blocks):
        part = slice(block * rows, (block + 1) * rows)
        scale = scale_of(part)
        keys = rotated(acc_kv[part, :HEAD_DIM] * scale, cos[part, :], sin[part, :])
        values = acc_kv[part, HEAD_DIM:] * scale
        pieces.append(jnp.concatenate([keys.astype(BF16), values.astype(BF16)], axis=1))
    both = jnp.dot(sel[...], jnp.concatenate(pieces, axis=0), preferred_element_type=F32)
    kv_out[0] = both[:, :HEAD_DIM].astype(BF16)
    kv_out[1] = both[:, HEAD_DIM:].astype(BF16)

    copies_w[2].wait()
    heads = wq.shape[1] // HEAD_DIM
    factor = HEAD_DIM ** (-0.5) * 1.4426950408889634

    @pl.loop(0, blocks)
    def _(block):
        part = pl.ds(pl.multiple_of(block * rows, rows), rows)
        product = jnp.dot(xg[part, :], wqv[...], preferred_element_type=F32)
        scale = scale_of(part) * factor
        for head in range(heads):
            lanes = slice(head * HEAD_DIM, (head + 1) * HEAD_DIM)
            turned = rotated(product[:, lanes] * scale, cos[part, :], sin[part, :])
            acc_q[part, lanes] = turned.astype(BF16)

    picked = jnp.dot(sel[...], acc_q[...], preferred_element_type=F32)
    for head in range(heads):
        q_out[head] = picked[:, head * HEAD_DIM : (head + 1) * HEAD_DIM].astype(BF16)


def smem():
    return pl.BlockSpec(memory_space=pltpu.SMEM)


def vmem():
    return pl.BlockSpec(memory_space=pltpu.VMEM)


def hbm():
    return pl.BlockSpec(memory_space=pl.ANY)


def front(shard, counts, pos, gain, big, small, hidden, wq, wk, wv):
    seq, width = hidden.shape
    slots = pos.shape[1]
    heads = wq.shape[1] // HEAD_DIM
    return pl.pallas_call(
        front_kernel,
        out_shape=(
            jax.ShapeDtypeStruct((heads, slots, HEAD_DIM), BF16),
            jax.ShapeDtypeStruct((2, slots, HEAD_DIM), BF16),
        ),
        in_specs=[smem(), smem(), vmem(), vmem(), vmem(), vmem(), hbm(), hbm(), hbm(), hbm()],
        out_specs=(vmem(), vmem()),
        scratch_shapes=[
            pltpu.VMEM((3, seq, CHUNK), BF16),
            pltpu.VMEM((width, 2 * HEAD_DIM), BF16),
            pltpu.VMEM(wq.shape, BF16),
            pltpu.VMEM((seq, width), BF16),
            pltpu.VMEM((seq, 2 * HEAD_DIM), F32),
            pltpu.VMEM((seq, heads * HEAD_DIM), BF16),
            pltpu.VMEM((seq, 128), F32),
            pltpu.VMEM((seq, HEAD_DIM), F32),
            pltpu.VMEM((seq, HEAD_DIM), F32),
            pltpu.VMEM((slots, seq), BF16),
            pltpu.SemaphoreType.DMA((3,)),
            pltpu.SemaphoreType.DMA((3,)),
        ],
        compiler_params=pltpu.CompilerParams(vmem_limit_bytes=VMEM_LIMIT),
        name="front",
    )(shard, counts, pos, gain, big, small, hidden, wq, wk, wv)


def attend_kernel(shard_ref, live_ref, q_ref, kv_ref, out_ref, keys, values, best, acc):
    shards, _, slots, dim = kv_ref.shape
    heads = q_ref.shape[0]
    me = shard_ref[0]
    lane = lax.broadcasted_iota(jnp.int32, (slots, dim), 1)
    row = lax.broadcasted_iota(jnp.int32, (slots, dim), 0)

    def place(shard, start):
        live = live_ref[shard]
        part = pl.ds(pl.multiple_of(start, 16), slots)
        keys[part, :dim] = kv_ref[shard, 0]
        keys[part, dim:] = jnp.where((lane == 0) & (row >= live), -1e30, 0.0).astype(BF16)
        values[part, :] = kv_ref[shard, 1]
        return start + (live + 15) // 16 * 16

    own = lax.fori_loop(0, me, place, jnp.int32(0))
    place(me, own)
    full = own // KEY_CHUNK
    tile = 128
    ones = jnp.where(lane == 0, 1.0, 0.0).astype(BF16)
    lane_q = lax.broadcasted_iota(jnp.int32, (heads * tile, dim), 1)
    ones_q = jnp.where(lane_q == 0, 1.0, 0.0).astype(BF16)
    tail = pl.ds(pl.multiple_of(own + slots, 16), KEY_CHUNK)
    keys[tail, :dim] = jnp.zeros((KEY_CHUNK, dim), BF16)
    keys[tail, dim:] = jnp.where(lane == 0, -1e30, 0.0).astype(BF16)
    values[tail, :] = jnp.zeros((KEY_CHUNK, dim), BF16)

    @pl.loop(0, (live_ref[me] + tile - 1) // tile)
    def _(block):
        rows = pl.ds(pl.multiple_of(block * tile, tile), tile)
        query = jnp.concatenate([q_ref[head, rows, :] for head in range(heads)], axis=0)
        query = jnp.concatenate([query, ones_q], axis=1)
        best[...] = jnp.full_like(best, -3e38)
        acc[...] = jnp.zeros_like(acc)

        def step(chunk, masked):
            part = pl.ds(pl.multiple_of(chunk * KEY_CHUNK, KEY_CHUNK), KEY_CHUNK)
            score = lax.dot_general(
                query, keys[part, :], (((1,), (1,)), ((), ())), preferred_element_type=F32
            )
            if masked:
                key_at = lax.broadcasted_iota(jnp.int32, score.shape, 1) + chunk * KEY_CHUNK
                query_at = lax.broadcasted_iota(jnp.int32, score.shape, 0)
                limit = jnp.bitwise_and(query_at, tile - 1) + (own + block * tile)
                score = jnp.where(key_at <= limit, score, -1e30)
            old = best[...]
            new = jnp.maximum(old, jnp.max(score, axis=1, keepdims=True))
            weight = jnp.exp2(score - new[:, :1]).astype(BF16)
            both = jnp.concatenate([values[part, :], ones], axis=1)
            product = jnp.dot(weight, both, preferred_element_type=F32)
            factor = jnp.exp2(old - new)
            acc[:, :dim] = acc[:, :dim] * factor + product[:, :dim]
            acc[:, dim:] = acc[:, dim:] * factor + product[:, dim:]
            best[...] = new

        @pl.loop(0, full)
        def _(chunk):
            step(chunk, False)

        last = (own + (block + 1) * tile + KEY_CHUNK - 1) // KEY_CHUNK

        @pl.loop(full, last)
        def _(chunk):
            step(chunk, True)

        total = acc[:, dim : dim + 1]
        result = acc[:, :dim] / total
        for head in range(heads):
            out_ref[rows, head * dim : (head + 1) * dim] = result[
                head * tile : (head + 1) * tile, :
            ].astype(BF16)


def attend(shard, live, q, kv):
    heads, slots, dim = q.shape
    shards = kv.shape[0]
    length = shards * slots + KEY_CHUNK + 512
    return pl.pallas_call(
        attend_kernel,
        out_shape=jax.ShapeDtypeStruct((slots, heads * dim), BF16),
        in_specs=[smem(), smem(), vmem(), vmem()],
        out_specs=vmem(),
        scratch_shapes=[
            pltpu.VMEM((length, 2 * dim), BF16),
            pltpu.VMEM((length, dim), BF16),
            pltpu.VMEM((heads * 128, 128), F32),
            pltpu.VMEM((heads * 128, 2 * dim), F32),
        ],
        compiler_params=pltpu.CompilerParams(vmem_limit_bytes=VMEM_LIMIT),
        name="attend",
    )(shard, live, q, kv)


def merge_kernel(shard_ref, counts_ref, pos_ref, router_ref, parts_ref, own_ref, out_ref, sel):
    seq, width = own_ref.shape
    members, slots, _ = parts_ref.shape
    sel[...] = select_matrix(counts_ref, pos_ref, shard_ref[0] * seq, slots, seq)
    total = parts_ref[0].astype(F32)
    for member in range(1, members):
        total = total + parts_ref[member].astype(F32)
    live = lax.broadcasted_iota(jnp.int32, (slots, width), 0) < live_rows(
        counts_ref, slots // BLOCK
    )
    total = jnp.where(live, total, 0.0)
    high = total.astype(BF16)
    low = (total - high.astype(F32)).astype(BF16)
    dims = (((0,), (0,)), ((), ()))
    update = lax.dot_general(sel[...], high, dims, preferred_element_type=F32)
    update = update + lax.dot_general(sel[...], low, dims, preferred_element_type=F32)
    router = jnp.transpose(jnp.broadcast_to(router_ref[...], (128, seq)))[:, :1]
    out_ref[...] = (own_ref[...].astype(F32) + router * update).astype(BF16)


def merge(shard, counts, pos, router, parts, own):
    return pl.pallas_call(
        merge_kernel,
        out_shape=jax.ShapeDtypeStruct(own.shape, BF16),
        in_specs=[smem(), smem(), vmem(), vmem(), vmem(), vmem()],
        out_specs=vmem(),
        scratch_shapes=[pltpu.VMEM((pos.shape[1], own.shape[0]), BF16)],
        compiler_params=pltpu.CompilerParams(vmem_limit_bytes=VMEM_LIMIT),
        name="merge",
    )(shard, counts, pos, router, parts, own)


def per_device(
    hidden, norm_gain, w_query, w_key, w_value, w_output, positions, counts, router_weight
):
    seq = hidden.shape[0]
    slots = positions.shape[0]
    shards = lax.axis_size(CTX)
    shard = lax.axis_index(CTX).astype(jnp.int32)
    big, small = angle_tables(seq, shards)
    big = lax.dynamic_index_in_dim(jnp.asarray(big), shard, 0, keepdims=False)
    shard = shard.reshape(1)
    pos = positions.reshape(1, slots)
    q, kv = front(
        shard, counts, pos, norm_gain.reshape(1, -1), big, jnp.asarray(small),
        hidden, w_query, w_key, w_value,
    )
    live = lax.all_gather(jnp.sum(counts), CTX, axis=0)
    gathered = lax.all_gather(kv, CTX, axis=0)
    attn = attend(shard, live, q, gathered)
    product = jnp.dot(attn, w_output, preferred_element_type=F32).astype(BF16)
    members = lax.axis_size(TP)
    width = product.shape[1] // members
    parts = jnp.moveaxis(product.reshape(slots, members, width), 1, 0)
    arrived = lax.all_to_all(parts, TP, split_axis=0, concat_axis=0, tiled=True)
    own = lax.dynamic_slice_in_dim(hidden, lax.axis_index(TP) * width, width, 1)
    return merge(shard, counts, pos, router_weight.reshape(1, seq), arrived, own)


def solution(mesh):
    finer = Mesh(mesh.devices.reshape(2, 4, 2, 4, 2), CTX + TP)
    return jax.shard_map(
        per_device,
        mesh=finer,
        in_specs=(
            P(CTX, None), P(), P(None, TP), P(None, TP), P(None, TP), P(TP, None),
            P(CTX), P(CTX), P(CTX),
        ),
        out_specs=P(CTX, TP),
        check_vma=False,
    )
```

time: 391 us -> 203 us (0.52)
  matrix products: 142 us -> 6.64 us
  Pallas kernels: 0 us -> 71.8 us
  other arithmetic: 66.4 us -> 0.65 us
  blocking collectives: 34.5 us -> 8.92 us
  waiting for transfers between devices: 98.8 us -> 73.6 us
  local copies, waits for them, and re-layouts: 26.9 us -> 18.7 us
    dot_general x36 -> x1, matrix products: 142 us -> 6.64 us  [per_device(): product = jnp.dot(attn, w_output, preferred_element_type=F32).astype(BF16)]
    pallas_call x0 -> x3, Pallas kernels: none -> 71.8 us  [the longest x1 49.9 us: attend(): pl.pallas_call(attend_kernel, out_shape=jax.ShapeDtypeStruct((slots, head...]
    all_gather x5 -> x0, blocking collectives: 34.5 us -> none  [gathered_by_axis(): nearer = lax.all_gather(value, axes[-1], axis=dim, tiled=True)]
    all_to_all x1, waiting for transfers between devices: 56.3 us -> 30.5 us  [per_device(): arrived = lax.all_to_all(parts, TP, split_axis=0, concat_axis=0, tiled=True)]
    reduce_sum x18 -> x1, other arithmetic: 24.2 us -> 0.65 us  [per_device(): live = lax.all_gather(jnp.sum(counts), CTX, axis=0)]
    add x17 -> x0, other arithmetic: 20.3 us -> none  [the longest x16 20.3 us: block_step(): total = total * factor + jnp.sum(weight, axis=-1)]
    gather x3 -> x0, local copies, waits for them, and re-layouts: 16.8 us -> none  [the longest x1 13 us: per_device(): rows = hidden[index].astype(jnp.float32) * live[:, None].astype(jnp.float32)]
    unnamed x0 -> x1, blocking collectives: none -> 8.92 us
  transfers between devices with their start and end apart: 5 -> 2, of which waited for: 4 -> 2; matrix products, arithmetic and copies ran while one was open for 4% -> 2% of each run, Pallas kernels for 0% -> 0%
where the time goes in v1:
time: 203 us; the launch traced here: 200 us
  waiting for transfers between devices  73.6 us (36%)
  Pallas kernels  71.8 us (35%)
  local copies, waits for them, and re-layouts  18.7 us (9%)
  between operations  13.4 us (7%)
  blocking collectives  8.92 us (4%)
  matrix products  6.64 us (3%)
  starting transfers between devices  5.85 us (3%)
    pallas_call x1, Pallas kernels, attend(): pl.pallas_call(attend_kernel, out_shape=jax.ShapeDtypeStruct((slots, head...  49.9 us
    all_gather x1, waiting for transfers between devices, per_device(): gathered = lax.all_gather(kv, CTX, axis=0)  43.1 us
    all_to_all x1, waiting for transfers between devices, per_device(): arrived = lax.all_to_all(parts, TP, split_axis=0, concat_axis=0, tiled=True)  30.5 us
    pallas_call x1, Pallas kernels, front(): pl.pallas_call(front_kernel, out_shape=(jax.ShapeDtypeStruct((heads, slot...  16.3 us
    unnamed x1, blocking collectives  8.92 us
    dot_general x1, matrix products, per_device(): product = jnp.dot(attn, w_output, preferred_element_type=F32).astype(BF16)  6.64 us
    reshape x1, local copies, waits for them, and re-layouts, per_device(): parts = jnp.moveaxis(product.reshape(slots, members, width), 1, 0)  6.5 us
    convert_element_type x1, local copies, waits for them, and re-layouts, per_device(): product = jnp.dot(attn, w_output, preferred_element_type=F32).astype(BF16)  6.47 us
  transfers between devices with their start and end apart: 2, of which 2 were waited for; matrix products, arithmetic and copies ran while one was open for 2% of the time, Pallas kernels for 0%

profile of v1, /device:TPU:88, one launch (start us, length us, event | category | flops | bytes accessed | tf_op | source)
XLA Modules:
  0.0 199.6 jit_solution(9735742911646805837)
XLA Ops:
  6.5 0.0 all-gather.3.cloned.1.call-start
  6.5 1.4 dynamic-slice_bitcast_fusion.big_ref
  7.9 0.0 copy-start
  7.9 0.0 copy-start.1
  7.9 16.3 %front.1 = (bf16[4,512,128]{2,1,0:T(8,128)(2,1)}, bf16[2,512,128]{2,1,0:T(8,128)(2,1)}) custom-call(s32[1]{0:T(128)} %bitcast.shard_ref, s32[4]{0:T(128)} %counts_ref.3, s32[1,512]{1,0:T(1,128)} %bitcast.17, f32[1,4096]{1,0:T(1,128)} %bitcast.16, f32[2,32,128]{2,1,0:T(8,128)} %dynamic-slice_bitcast_fusion.big_ref, f32[3,32,128]{2,1,0:T(8,128)} %constant.39.clone.small_ref, ...), custom_call_target="tpu_custom_call" | custom-call | tf_op jit(solution)/shard_map/front/pallas_call | solution.py:185
  24.2 0.0 all-gather.3.cloned.1.call-update
  24.2 0.0 copy-done
  24.2 0.6 reduce_sum.9
  24.9 0.0 copy-done.1
  24.9 0.6 dynamic-slice
  25.5 1.4 dynamic-update-slice
  26.8 8.9 %all-reduce.live_ref = s32[16]{0:T(128)} all-reduce(s32[16]{0:T(128)S(1)} %dynamic-update-slice), channel_id=1, replica_groups=mesh['zh'=2,'y'=4,'core'=2,'x'=4,'zl'=2] {'zh','y','core'}, use_global_device_ids=true, to_apply=%add | all-reduce | flops 16 | bytes 128
  35.8 43.1 %all-gather.3.cloned.1.call-done = bf16[32,512,128]{2,1,0:T(8,128)(2,1)} async-done(((bf16[2,512,128]{2,1,0:T(8,128)(2,1)}), bf16[32,512,128]{2,1,0:T(8,128)(2,1)}) %all-gather.3.cloned.1.call-update) | async-done | bytes 4194320 | tf_op jit(solution)/shard_map/all_gather | solution.py:353
  78.9 49.9 %attend.1 = bf16[512,512]{1,0:T(8,128)(2,1)} custom-call(s32[1]{0:T(128)} %bitcast.shard_ref, s32[16]{0:T(128)} %all-reduce.live_ref, bf16[4,512,128]{2,1,0:T(8,128)(2,1)} %get-tuple-element.7.q_ref, bf16[16,2,512,128]{3,2,1,0:T(8,128)(2,1)} %bitcast.15), custom_call_target="tpu_custom_call" | custom-call | tf_op jit(solution)/shard_map/attend/pallas_call | solution.py:289
  128.8 6.6 %convolution_convert_fusion = bf16[512,4096]{1,0:T(8,128)(2,1)} fusion(bf16[512,512]{1,0:T(8,128)(2,1)} %attend.1, bf16[512,4096]{1,0:T(8,128)(2,1)} %param.16), kind=kOutput, calls=%fused_computation | convolution fusion | flops 2149580800 | bytes 8912896 | tf_op jit(solution)/shard_map/dot_general | solution.py:355
  135.4 6.5 %copy.14 = bf16[512,4096]{0,1:T(8,128)(2,1)} copy(bf16[512,4096]{1,0:T(8,128)(2,1)} %convolution_convert_fusion) | data formatting | bytes 8388608 | tf_op jit(solution)/shard_map/convert_element_type | solution.py:355
  141.9 6.5 %copy.15 = bf16[512,8,512]{2,0,1:T(8,128)(2,1)} copy(bf16[512,8,512]{0,2,1:T(8,128)(2,1)} %bitcast.14) | data formatting | bytes 8388608 | tf_op jit(solution)/shard_map/reshape | solution.py:358
  148.4 5.8 %all-to-all-start = ((bf16[8,512,512]{2,1,0:T(8,128)(2,1)}), bf16[8,512,512]{2,1,0:T(8,128)(2,1)}, u32[]{:S(2)}, u32[]{:S(2)}) async-start(bf16[8,512,512]{2,1,0:T(8,128)(2,1)} %bitcast.13), calls=%async_computation | async-start | bytes 8388608 | tf_op jit(solution)/shard_map/all_to_all | solution.py:359
  154.3 2.3 %constant_dynamic-slice_fusion.own_ref = bf16[1024,512]{1,0:T(8,128)(2,1)} fusion(bf16[1024,4096]{1,0:T(8,128)(2,1)} %hidden.1, s32[]{:T(128)S(6)} %select_n.8), kind=kLoop, calls=%fused_computation.2 | loop fusion | bytes 2097156 | tf_op jit(solution)/shard_map/dynamic_slice | solution.py:360
  156.6 30.5 %all-to-all-done.parts_ref = bf16[8,512,512]{2,1,0:T(8,128)(2,1)} async-done(((bf16[8,512,512]{2,1,0:T(8,128)(2,1)}), bf16[8,512,512]{2,1,0:T(8,128)(2,1)}, u32[]{:S(2)}, u32[]{:S(2)}) %all-to-all-start) | async-done | bytes 4194336 | tf_op jit(solution)/shard_map/all_to_all | solution.py:359
  187.1 5.6 %merge.1 = bf16[1024,512]{1,0:T(8,128)(2,1)} custom-call(s32[1]{0:T(128)} %bitcast.shard_ref, s32[4]{0:T(128)} %counts_ref.3, s32[1,512]{1,0:T(1,128)} %bitcast.18, f32[1,1024]{1,0:T(1,128)} %bitcast.19, bf16[8,512,512]{2,1,0:T(8,128)(2,1)} %all-to-all-done.parts_ref, bf16[1024,512]{1,0:T(8,128)(2,1)} %constant_dynamic-slice_fusion.own_ref), custom_call_target="tpu_custom_call" | custom-call | tf_op jit(solution)/shard_map/merge/pallas_call | solution.py:326
  (1 shorter events, 0.0 us)
Async XLA Ops:
  6.5 72.3 %all-gather.3.cloned.1.call-start = ((), (), s32[]{:S(2)}) async-start(), calls=%async_computation.1 | async-start | bytes 4456448 | tf_op jit(solution)/shard_map/all_gather | solution.py:353
  7.9 16.3 %copy-start = (s32[4]{0:T(128)S(1)}, s32[4]{0:T(128)}, u32[]{:S(2)}) copy-start(s32[4]{0:T(128)} %counts_ref.3) | copy-start | bytes 52
  7.9 17.0 %copy-start.1 = (u32[128]{0:T(128)S(1)}, u32[128]{0:T(128)}, u32[]{:S(2)}) copy-start(u32[128]{0:T(128)} %constant.43) | copy-start | bytes 1540
  148.4 38.7 %all-to-all-start = ((bf16[8,512,512]{2,1,0:T(8,128)(2,1)}), bf16[8,512,512]{2,1,0:T(8,128)(2,1)}, u32[]{:S(2)}, u32[]{:S(2)}) async-start(bf16[8,512,512]{2,1,0:T(8,128)(2,1)} %bitcast.13), calls=%async_computation | async-start | bytes 8388608 | tf_op jit(solution)/shard_map/all_to_all | solution.py:359
Sparse Core Ops, SparseCore 0:
  24.3 54.4 all-gather.2
